TPU v7x, 32 devices: a whole 2x2x4 slice. The times are simulated.
32 devices in a mesh: rep: 4 (over y, x), shard: 8 (over z, core).
Axes of the slice: x: 2, y: 2, z: 4, core: 2. Of those that a mesh axis runs over, the one named last changes fastest.
Arguments:
- hot_ids: int32 [65536], P(('rep', 'shard')), may hold values from 0 to 8191
- hot_grads: bfloat16 [65536, 128], P(('rep', 'shard')), may hold values from -6 to 6
- hot_rows: float32 [8192, 128], replicated, may hold values from -6 to 6
- hot_accum: float32 [8192], replicated, may hold values from 0.5 to 4
- cold_counts: int32 [32, 32], P(('rep', 'shard')), may hold values from 1 to 16, as said below
- cold_slots: int32 [32, 32, 16], P(('rep', 'shard')), may hold values from 0 to 8191
- cold_grads: bfloat16 [32, 32, 16, 128], P(('rep', 'shard')), may hold values from -6 to 6
- cold_rows: float32 [262144, 128], P(('rep', 'shard')), may hold values from -6 to 6
- cold_accum: float32 [262144], P(('rep', 'shard')), may hold values from 0.5 to 4
Outputs:
- new_hot_rows: float32 [8192, 128], replicated
- new_hot_accum: float32 [8192], replicated
- new_cold_rows: float32 [262144, 128], P(('rep', 'shard'))
- new_cold_accum: float32 [262144], P(('rep', 'shard'))
Inputs may be any that keep to these rules, and one draw needn't show every extreme that they name: `cold_counts`: every entry is at least 1 and at most 16; in every draw some owner receives 16 live slots from every sender.
All inputs are finite; a program needn't handle non-finite values.
Results may differ from a plain program's by a relative error of at most 0.0003.
Values may be sent and summed in bfloat16 or wider, within the bound.
A program may use at most 128 MiB of HBM per device.

v0:
```python
import jax
import jax.numpy as jnp
from jax import lax
from jax.sharding import PartitionSpec as P

learn_rate = 0.5


def adagrad(table_rows, accum_rows, gradient):
    accum_new = accum_rows + jnp.mean(gradient * gradient, axis=1)
    return (table_rows - learn_rate * gradient / jnp.sqrt(accum_new)[:, None], accum_new)


def local(
    hot_ids,
    hot_grads,
    hot_rows,
    hot_accum,
    cold_counts,
    cold_slots,
    cold_grads,
    cold_rows,
    cold_accum,
):
    hot_count = hot_rows.shape[0]
    dense = jax.ops.segment_sum(hot_grads.astype(jnp.float32), hot_ids, num_segments=hot_count)
    share = hot_count // lax.axis_size("shard")
    part_sum = lax.psum_scatter(dense, "shard", scatter_dimension=0, tiled=True)
    part_sum = lax.psum(part_sum, "rep")
    start = lax.axis_index("shard") * share
    rows_share = lax.dynamic_slice_in_dim(hot_rows, start, share, 0)
    accum_share = lax.dynamic_slice_in_dim(hot_accum, start, share, 0)
    rows_new, accum_new = adagrad(rows_share, accum_share, part_sum)
    new_hot_rows, new_hot_accum = (
        lax.all_gather(rows_new, "shard", axis=0, tiled=True),
        lax.all_gather(accum_new, "shard", axis=0, tiled=True),
    )
    received, slots_in, counts_in = (
        lax.all_to_all(cold_grads, ("rep", "shard"), split_axis=1, concat_axis=0, tiled=True),
        lax.all_to_all(cold_slots, ("rep", "shard"), split_axis=1, concat_axis=0, tiled=True),
        lax.all_to_all(cold_counts, ("rep", "shard"), split_axis=1, concat_axis=0, tiled=True),
    )
    width = received.shape[-1]
    capacity = received.shape[2]
    slot_index = lax.broadcasted_iota(jnp.int32, (1, 1, capacity), 2)
    live_mask = slot_index < counts_in[:, :, None]
    masked_terms = jnp.where(live_mask[..., None], received.astype(jnp.float32), 0.0)
    local_rows = cold_rows.shape[0]
    cold_sum = jax.ops.segment_sum(
        masked_terms.reshape(-1, width), slots_in.reshape(-1), num_segments=local_rows
    )
    new_cold_rows, new_cold_accum = adagrad(cold_rows, cold_accum, cold_sum)
    return (new_hot_rows, new_hot_accum, new_cold_rows, new_cold_accum)


def solution(mesh):
    placed = (
        P(("rep", "shard")),
        P(("rep", "shard"), None),
        P(),
        P(),
        P(("rep", "shard"), None),
        P(("rep", "shard"), None, None),
        P(("rep", "shard"), None, None, None),
        P(("rep", "shard"), None),
        P(("rep", "shard")),
    )
    return jax.shard_map(
        local,
        mesh=mesh,
        in_specs=placed,
        out_specs=(P(), P(), P(("rep", "shard"), None), P(("rep", "shard"))),
        check_vma=False,
    )
```

profile of v0, /device:TPU:0, one launch (start us, length us, event | category | flops | bytes accessed | tf_op | source)
XLA Modules:
  0.0 199.6 jit_solution(5830766798041887270)
XLA Ops:
  7.2 0.0 reduce-scatter.2.cloned.1.call-start
  7.2 14.1 %scatter_custom_fusion = f32[8192,128]{1,0:T(8,128)} fusion(s32[2048]{0:T(1024)} %param.9, f32[]{:T(128)} %constant.3.clone.1, bf16[2048,128]{1,0:T(8,128)(2,1)} %param.10), kind=kCustom, calls=%fused_computation.6 | custom fusion | flops 524288 | bytes 4719104 | tf_op jit(solution)/shard_map/scatter-add | solution.py:26
  21.3 0.0 reduce-scatter.2.cloned.1.call-update
  21.3 0.0 all-reduce.2.cloned.1.call-start
  21.4 52.8 %reduce-scatter.2.cloned.1.call-done = f32[1024,128]{1,0:T(8,128)} async-done(((f32[8192,128]{1,0:T(8,128)}), f32[1024,128]{1,0:T(8,128)}) %reduce-scatter.2.cloned.1.call-update) | async-done | bytes 524304 | tf_op jit(solution)/shard_map/reduce_scatter | solution.py:28
  74.1 0.0 all-reduce.2.cloned.1.call-update
  74.2 0.0 all-gather.2.cloned.1.call-start
  74.2 46.8 %all-reduce.2.cloned.1.call-done = f32[1024,128]{1,0:T(8,128)} async-done(((f32[1024,128]{1,0:T(8,128)}), f32[1024,128]{1,0:T(8,128)}) %all-reduce.2.cloned.1.call-update) | async-done | bytes 524304 | tf_op jit(solution)/shard_map/psum | solution.py:29
  121.0 1.2 multiply_reduce_fusion.1
  122.2 0.7 fusion.8
  122.9 2.2 %divide_subtract_fusion.1 = f32[1024,128]{1,0:T(8,128)} fusion(f32[1024,128]{1,0:T(8,128)} %all-reduce.2.cloned.1.call-done, f32[8192,128]{1,0:T(8,128)} %param.11, s32[]{:T(128)S(6)} %select_n.11, f32[1024]{0:T(1024)S(1)} %get-tuple-element.6), kind=kLoop, calls=%fused_computation.9 | loop fusion | flops 393216 | bytes 1576964 | tf_op jit(solution)/shard_map/sub | solution.py:11
  125.1 0.0 all-gather.2.cloned.1.call-update
  125.2 0.7 copy.18
  125.9 4.6 %all-to-all-start.1 = ((s32[1,32,1]{2,0,1:T(1,128)}), s32[1,32,1]{2,0,1:T(1,128)S(1)}, u32[]{:S(2)}, u32[]{:S(2)}) async-start(s32[1,32,1]{2,0,1:T(1,128)} %copy.18), calls=%async_computation.2 | async-start | bytes 32768 | tf_op jit(solution)/shard_map/all_to_all | solution.py:41
  130.5 0.1 copy.17
  130.6 7.0 %all-to-all-done.1 = s32[1,32,1]{2,0,1:T(1,128)S(1)} async-done(((s32[1,32,1]{2,0,1:T(1,128)}), s32[1,32,1]{2,0,1:T(1,128)S(1)}, u32[]{:S(2)}, u32[]{:S(2)}) %all-to-all-start.1) | async-done | bytes 160 | tf_op jit(solution)/shard_map/all_to_all | solution.py:41
  137.6 9.1 %all_to_all.31 = s32[1,32,16]{2,0,1:T(1,128)S(1)} all-to-all(s32[1,32,16]{2,0,1:T(1,128)S(1)} %copy.17), channel_id=1, replica_groups=mesh['rep'=4,'shard'=8] {'rep','shard'}, dimensions={1} | all-to-all | bytes 4096 | tf_op jit(solution)/shard_map/all_to_all | solution.py:40
  146.7 2.6 %all-to-all-start.2 = ((bf16[1,32,16,128]{3,2,0,1:T(8,128)(2,1)}), bf16[1,32,16,128]{3,2,0,1:T(8,128)(2,1)S(1)}, u32[]{:S(2)}, u32[]{:S(2)}) async-start(bf16[1,32,16,128]{3,2,0,1:T(8,128)(2,1)} %bitcast.1), calls=%async_computation.3 | async-start | bytes 262144 | tf_op jit(solution)/shard_map/all_to_all | solution.py:39
  149.3 0.7 reduce.1
  150.0 0.1 iota_compare_fusion
  150.0 0.1 lt.33
  150.1 0.5 broadcast.40
  150.6 0.7 reduce.4
  151.3 0.1 reshape.77
  151.4 9.5 %all-to-all-done.2 = bf16[1,32,16,128]{3,2,0,1:T(8,128)(2,1)S(1)} async-done(((bf16[1,32,16,128]{3,2,0,1:T(8,128)(2,1)}), bf16[1,32,16,128]{3,2,0,1:T(8,128)(2,1)S(1)}, u32[]{:S(2)}, u32[]{:S(2)}) %all-to-all-start.2) | async-done | bytes 131104 | tf_op jit(solution)/shard_map/all_to_all | solution.py:39
  160.9 4.6 %scatter_custom_fusion.1 = f32[8192,128]{1,0:T(8,128)} fusion(s32[512]{0:T(512)S(1)} %reshape.77, f32[]{:T(128)} %constant.3.clone.1, bf16[512,128]{1,0:T(8,128)(2,1)S(1)} %bitcast.7, pred[512]{0:T(512)(128)(4,1)S(1)} %lt.33), kind=kCustom, calls=%fused_computation.4 | custom fusion | flops 196608 | bytes 4326912 | tf_op jit(solution)/shard_map/scatter-add | solution.py:49
  165.5 3.5 %multiply_reduce_fusion = f32[8192]{0:T(1024)S(1)} fusion(f32[8192,128]{1,0:T(8,128)} %scatter_custom_fusion.1), kind=kLoop, calls=%fused_computation.3 | loop fusion | flops 2088960 | bytes 4227072 | tf_op jit(solution)/shard_map/reduce_sum | solution.py:10
  169.1 0.6 fusion.7
  169.7 4.2 %divide_subtract_fusion = f32[8192,128]{1,0:T(8,128)} fusion(f32[8192,128]{1,0:T(8,128)} %param.16, f32[8192,128]{1,0:T(8,128)S(1)} %copy-done, f32[8192]{0:T(1024)S(1)} %get-tuple-element.4), kind=kLoop, calls=%fused_computation.2 | loop fusion | flops 3145728 | bytes 12615680 | tf_op jit(solution)/shard_map/sub | solution.py:11
  173.9 14.1 %all_gather.7 = f32[8192]{0:T(1024)S(1)} all-gather(f32[1024]{0:T(1024)S(1)} %get-tuple-element.7), channel_id=1, replica_groups=mesh['rep'=4,'shard'=8] {'shard'}, dimensions={0}, use_global_device_ids=true | all-gather | bytes 36864 | tf_op jit(solution)/shard_map/all_gather | solution.py:36
  188.0 4.5 %copy.23 = f32[8192,128]{1,0:T(8,128)} copy(f32[8192,128]{1,0:T(8,128)} %all-gather.2.cloned.1.call-done) | data formatting | bytes 8388608
  192.4 0.6 copy.24
  (9 shorter events, 0.0 us)
Async XLA Ops:
  7.2 67.0 %reduce-scatter.2.cloned.1.call-start = ((), (), s32[]{:S(2)}) async-start(), calls=%async_computation.4 | async-start | bytes 4718592 | tf_op jit(solution)/shard_map/reduce_scatter | solution.py:28
  21.3 103.9 %copy-start.3 = (s32[1,32]{1,0:T(1,128)S(1)}, s32[1,32]{1,0:T(1,128)}, u32[]{:S(2)}) copy-start(s32[1,32]{1,0:T(1,128)} %param.13) | copy-start | bytes 388
  21.3 109.2 %copy-start.2 = (s32[1,32,16]{1,2,0:T(8,128)S(1)}, s32[1,32,16]{1,2,0:T(8,128)}, u32[]{:S(2)}) copy-start(s32[1,32,16]{1,2,0:T(8,128)} %param.14) | copy-start | bytes 6148
  21.3 99.7 %all-reduce.2.cloned.1.call-start = ((), (), s32[]{:S(2)}) async-start(), calls=%async_computation.5 | async-start | bytes 1048576 | tf_op jit(solution)/shard_map/psum | solution.py:29
  74.2 113.8 %all-gather.2.cloned.1.call-start = ((), (), s32[]{:S(2)}) async-start(), calls=%async_computation.6 | async-start | bytes 4718592 | tf_op jit(solution)/shard_map/all_gather | solution.py:35
  125.9 11.7 %all-to-all-start.1 = ((s32[1,32,1]{2,0,1:T(1,128)}), s32[1,32,1]{2,0,1:T(1,128)S(1)}, u32[]{:S(2)}, u32[]{:S(2)}) async-start(s32[1,32,1]{2,0,1:T(1,128)} %copy.18), calls=%async_computation.2 | async-start | bytes 32768 | tf_op jit(solution)/shard_map/all_to_all | solution.py:41
  146.7 14.2 %all-to-all-start.2 = ((bf16[1,32,16,128]{3,2,0,1:T(8,128)(2,1)}), bf16[1,32,16,128]{3,2,0,1:T(8,128)(2,1)S(1)}, u32[]{:S(2)}, u32[]{:S(2)}) async-start(bf16[1,32,16,128]{3,2,0,1:T(8,128)(2,1)} %bitcast.1), calls=%async_computation.3 | async-start | bytes 262144 | tf_op jit(solution)/shard_map/all_to_all | solution.py:39
  160.9 8.1 %copy-start.1 = (f32[8192]{0:T(1024)S(1)}, f32[8192]{0:T(1024)}, u32[]{:S(2)}) copy-start(f32[8192]{0:T(1024)} %param.17) | copy-start | bytes 98308
  165.5 4.1 %copy-start = (f32[8192,128]{1,0:T(8,128)S(1)}, f32[8192,128]{1,0:T(8,128)}, u32[]{:S(2)}) copy-start(f32[8192,128]{1,0:T(8,128)} %scatter_custom_fusion.1) | copy-start | bytes 12582916
Sparse Core Ops, SparseCore 0:
  21.4 52.6 reduce-scatter.1
  77.1 43.8 all-reduce.1
  125.3 50.0 all-gather.1
where the time goes:
time: 200 us
  waiting for transfers between devices  116 us (58%)
  other arithmetic  32.6 us (16%)
  blocking collectives  23.2 us (12%)
  between operations  13.8 us (7%)
  starting transfers between devices  7.29 us (4%)
  local copies, waits for them, and re-layouts  6.56 us (3%)
    reduce_scatter x1, waiting for transfers between devices, local(): part_sum = lax.psum_scatter(dense, 'shard', scatter_dimension=0, tiled=True)  52.8 us
    psum x1, waiting for transfers between devices, local(): part_sum = lax.psum(part_sum, 'rep')  46.8 us
    scatter-add x1, other arithmetic, local(): jax.ops.segment_sum(hot_grads.astype(jnp.float32), hot_ids, num_segments=...  14.1 us
    all_gather x1, blocking collectives, local(): lax.all_gather(accum_new, 'shard', axis=0, tiled=True)  14.1 us
    all_to_all x1, waiting for transfers between devices, local(): lax.all_to_all(cold_grads, ('rep', 'shard'), split_axis=1, concat_axis=0,...  9.51 us
    all_to_all x1, blocking collectives, local(): lax.all_to_all(cold_slots, ('rep', 'shard'), split_axis=1, concat_axis=0,...  9.13 us
    all_to_all x1, waiting for transfers between devices, local(): lax.all_to_all(cold_counts, ('rep', 'shard'), split_axis=1, concat_axis=0...  7.01 us
    sub x2, other arithmetic, adagrad(): table_rows - learn_rate * gradient / jnp.sqrt(accum_new)[:, None]  6.43 us
  transfers between devices with their start and end apart: 5, of which 4 were waited for; matrix products, arithmetic and copies ran while one was open for 8% of the time, Pallas kernels for 0%

commit v1 on v0

v1 whole, which is shorter than its diff:
```python
import functools

import jax
import jax.numpy as jnp
from jax import lax
from jax.experimental import pallas as pl
from jax.experimental.pallas import tpu as pltpu
from jax.sharding import PartitionSpec as P

learn_rate = 0.5
LANES = 128
PAD = 8
BOTH = ("rep", "shard")


def adagrad(rows, accum_row, grad):
    m = rows.shape[0]
    diag = lax.broadcasted_iota(jnp.int32, (m, LANES), 0) == lax.broadcasted_iota(
        jnp.int32, (m, LANES), 1
    )
    square = jnp.sum(grad * grad, axis=1, keepdims=True) * (1.0 / grad.shape[1])
    accum = jnp.sum(jnp.where(diag, accum_row, 0.0), axis=1, keepdims=True)
    accum_new = accum + square
    rows_new = rows - grad * (learn_rate / jnp.sqrt(accum_new))
    accum_new_row = jnp.sum(jnp.where(diag, accum_new, 0.0), axis=0, keepdims=True)
    return rows_new, accum_new_row


def onehot_dot(ids, base, rows, grads):
    lookups = ids.shape[1]
    row = lax.broadcasted_iota(jnp.int32, (rows, lookups), 0)
    hit = jnp.where(row == ids - base, 1.0, 0.0).astype(jnp.bfloat16)
    return jnp.dot(hit, grads, preferred_element_type=jnp.float32)


def kernel(
    reps, shards,
    ids, grads, hot_rows, hot_accum, cold_ids, cold_grads, cold_rows, cold_accum,
    hot_out, cold_out, cold_accum_out,
    ids_buf, grads_buf, acc, z_buf, rows_buf, cold_buf, cids_buf, cgrads_buf,
    raw_send, raw_recv, raw_core_send, raw_core_recv, z_send, z_recv,
    zg_send, zg_recv, rg_send, rg_recv, core_send, core_recv,
    cold_send, cold_recv, local_sem,
):
    total = reps * shards
    depth = shards // 2
    bits = reps.bit_length() - 1
    own_rows = acc.shape[1]
    half_rows = own_rows // 2
    rep, shard = lax.axis_index("rep"), lax.axis_index("shard")
    z, core = shard // 2, shard % 2
    me = rep * shards + shard
    partner = {"rep": rep, "shard": z * 2 + 1 - core}

    def flip(r, bit):
        m = 1 << bit
        return r + m * (1 - 2 * ((r // m) % 2))

    orders = (tuple(range(bits)), tuple(reversed(range(bits))))

    def origin(h, i):
        r = rep
        for k in range(bits):
            if (i >> k) & 1:
                r = flip(r, orders[h][k])
        return r

    def remote(src, dst, s_sem, r_sem, device):
        return pltpu.make_async_remote_copy(
            src_ref=src, dst_ref=dst, send_sem=s_sem, recv_sem=r_sem,
            device_id=device, device_id_type=pl.DeviceIdType.MESH,
        )

    chunk = (core * reps + rep) * depth + z
    loads = [
        pltpu.make_async_copy(cold_rows, cold_buf, local_sem.at[0]),
        pltpu.make_async_copy(hot_rows.at[pl.ds(2 * chunk, 2)], rows_buf, local_sem.at[1]),
        pltpu.make_async_copy(cold_ids.at[me], cids_buf.at[me], local_sem.at[2]),
        pltpu.make_async_copy(cold_grads.at[me], cgrads_buf.at[me], local_sem.at[3]),
    ]
    for copy in loads:
        copy.start()

    barrier = pltpu.get_barrier_semaphore()

    @pl.loop(1, total)
    def _(d):
        p = (me + d) % total
        pl.semaphore_signal(
            barrier, inc=1, device_id={"rep": p // shards, "shard": p % shards},
            device_id_type=pl.DeviceIdType.MESH,
        )

    pl.semaphore_wait(barrier, total - 1)

    sends = []
    arrivals = {}

    def raw_ref(h, i):
        if i == 0:
            return ids.at[h], grads.at[h]
        return ids_buf.at[0, h, i], grads_buf.at[0, h, i]

    def top(i):
        return i.bit_length() - 1

    def relay(h, i, q):
        j = i | (1 << q)
        device = {"rep": flip(rep, orders[h][q]), "shard": shard}
        pair = []
        for k, (src, buf) in enumerate(zip(raw_ref(h, i), (ids_buf, grads_buf))):
            slot = (h * reps + j) * 2 + k
            pair.append(remote(src, buf.at[0, h, j], raw_send.at[slot], raw_recv.at[slot], device))
        for copy in pair:
            copy.start()
            sends.append(copy)
        arrivals[h, j] = pair

    core_pairs = {}

    def cross(h, i):
        pair = []
        for k, (src, buf) in enumerate(zip(raw_ref(h, i), (ids_buf, grads_buf))):
            slot = (h * reps + i) * 2 + k
            pair.append(
                remote(src, buf.at[1, h, i], raw_core_send.at[slot], raw_core_recv.at[slot], partner)
            )
        for copy in pair:
            copy.start()
            sends.append(copy)
        core_pairs[h, i] = pair

    for q in range(bits):
        for h in range(2):
            relay(h, 0, q)
    for h in range(2):
        cross(h, 0)

    @pl.loop(1, total)
    def _(d):
        p = (me + d) % total
        device = {"rep": p // shards, "shard": p % shards}
        remote(cold_ids.at[p], cids_buf.at[me], cold_send.at[0], cold_recv.at[0], device).start()
        remote(cold_grads.at[p], cgrads_buf.at[me], cold_send.at[1], cold_recv.at[1], device).start()

    share = (core * reps + rep) * depth

    def block_sum(c, i, base):
        value = None
        for h in range(2):
            ids_ref, grads_ref = raw_ref(h, i) if c == 0 else (ids_buf.at[1, h, i], grads_buf.at[1, h, i])
            part = onehot_dot(ids_ref[...], base, own_rows, grads_ref[...])
            value = part if value is None else value + part
        return value

    def z_copy(d, zc):
        target = {"rep": rep, "shard": zc * 2 + core}
        return remote(acc.at[zc], z_buf.at[d - 1], z_send.at[d - 1], z_recv.at[d - 1], target)

    for i in range(reps):
        if i > 0:
            for h in range(2):
                for copy in arrivals[h, i]:
                    copy.wait_recv()
                for q in range(top(i) + 1, bits):
                    relay(h, i, q)
                cross(h, i)
        for c in range(2):
            if c == 1:
                for h in range(2):
                    for copy in core_pairs[h, i]:
                        copy.wait_recv()
            last = i == reps - 1 and c == 1

            @pl.loop(1, depth + 1)
            def _(d):
                zc = (z + d) % depth
                value = block_sum(c, i, (share + zc) * own_rows)
                if i == 0 and c == 0:
                    acc[zc] = value
                else:
                    acc[zc] += value
                if last:
                    @pl.when(d >= 2)
                    def _():
                        z_copy(d - 1, (z + d - 1) % depth).start()

    for copy in loads:
        copy.wait()
    for k, buf in enumerate((cids_buf, cgrads_buf)):
        part = buf.at[pl.ds(0, total - 1)]
        pltpu.make_async_copy(part, part, cold_recv.at[k]).wait()
    capacity = cgrads_buf.shape[1]
    group = LANES // capacity
    cold_id_row = jnp.concatenate(
        [jnp.sum(cids_buf[g * group:(g + 1) * group], axis=0) for g in range(total // group)], axis=1
    ) - 1

    step_rows = 2 * LANES

    @pl.loop(0, cold_buf.shape[0] // step_rows)
    def _(b):
        terms = cgrads_buf[...].reshape(total * capacity, LANES)
        grad = onehot_dot(cold_id_row, b * step_rows, step_rows, terms)
        for s in range(2):
            at = pl.ds(pl.multiple_of(b * step_rows + s * LANES, LANES), LANES)
            new_rows, new_accum = adagrad(
                cold_buf[at], cold_accum[2 * b + s], grad[s * LANES:(s + 1) * LANES]
            )
            cold_out[at] = new_rows
            cold_accum_out[2 * b + s] = new_accum

    @pl.loop(1, depth)
    def _(d):
        z_copy(d, (z + d) % depth).wait_recv()

    for h in range(2):
        at = pl.ds(h * half_rows, half_rows)
        grad = acc[z, at]
        for d in range(1, depth):
            grad += z_buf[d - 1, at]
        new_rows, new_accum = adagrad(rows_buf[h], hot_accum[2 * chunk + h], grad)
        hot_out[2 * chunk + h, pl.ds(0, half_rows)] = new_rows
        hot_out[2 * chunk + h, pl.ds(half_rows, PAD)] = jnp.broadcast_to(new_accum, (PAD, LANES))

    def zg_copy(d):
        target = {"rep": rep, "shard": ((z + d) % depth) * 2 + core}
        part = hot_out.at[pl.ds(2 * chunk, 2)]
        return remote(part, part, zg_send.at[d - 1], zg_recv.at[d - 1], target)

    for d in range(1, depth):
        zg_copy(d).start()

    gathered = {}

    def out_block(d, h, i):
        zc = (z + depth - d) % depth
        return hot_out.at[2 * ((core * reps + origin(h, i)) * depth + zc) + h]

    def spread(d, h, i):
        part = out_block(d, h, i)
        for q in range(top(i) + 1, bits):
            j = i | (1 << q)
            slot = (d * 2 + h) * reps + j
            device = {"rep": flip(rep, orders[h][q]), "shard": shard}
            copy = remote(part, part, rg_send.at[slot], rg_recv.at[slot], device)
            copy.start()
            sends.append(copy)
            gathered[d, h, j] = copy
        remote(part, part, core_send.at[0], core_recv.at[0], partner).start()

    def finish(d):
        for i in range(1, reps):
            for h in range(2):
                part = out_block(d, h, i)
                slot = (d * 2 + h) * reps + i
                remote(part, part, rg_send.at[slot], rg_recv.at[slot], partner).wait_recv()
                spread(d, h, i)

    for d in range(depth):
        if d > 0:
            zg_copy(d).wait_recv()
        for h in range(2):
            spread(d, h, 0)
        if d > 0:
            finish(d - 1)
    finish(depth - 1)

    for copy in sends:
        copy.wait_send()
    for d in range(1, depth):
        z_copy(d, (z + d) % depth).wait_send()
        zg_copy(d).wait_send()
    for k, buf in enumerate((cold_ids, cold_grads)):
        part = buf.at[pl.ds(0, total - 1)]
        pltpu.make_async_copy(part, part, cold_send.at[k]).wait()
    side = reps * depth * 2
    mine = hot_out.at[pl.ds(core * side, side)]
    other = hot_out.at[pl.ds((1 - core) * side, side)]
    pltpu.make_async_copy(mine, mine, core_send.at[0]).wait()
    pltpu.make_async_copy(other, other, core_recv.at[0]).wait()


def local(
    hot_ids, hot_grads, hot_rows, hot_accum, cold_counts, cold_slots, cold_grads, cold_rows, cold_accum
):
    reps, shards = lax.axis_size("rep"), lax.axis_size("shard")
    total, depth = reps * shards, shards // 2
    assert reps & (reps - 1) == 0 and shards % 2 == 0
    hot_count, width = hot_rows.shape
    lookups = hot_ids.shape[0]
    own_rows = hot_count // total
    half_rows = own_rows // 2
    cold_count = cold_rows.shape[0]
    capacity = cold_slots.shape[2]
    assert width == LANES and half_rows <= LANES and LANES % capacity == 0

    half = lookups // 2
    accum_blocks = hot_accum.reshape(2 * total, 1, half_rows)
    if half_rows < LANES:
        accum_blocks = jnp.pad(accum_blocks, ((0, 0), (0, 0), (0, LANES - half_rows)))
    group = LANES // capacity
    me = lax.axis_index("rep") * shards + lax.axis_index("shard")
    lane = lax.broadcasted_iota(jnp.int32, (total, 1, LANES), 2)
    live = (lane // capacity == me % group) & (lane % capacity < cold_counts.reshape(total, 1, 1))
    slot_lanes = jnp.tile(cold_slots.reshape(total, 1, capacity), (1, 1, group))
    cold_ids = jnp.where(live, slot_lanes + 1, 0)

    f32, i32, bf16 = jnp.float32, jnp.int32, jnp.bfloat16
    vmem, anywhere = pl.BlockSpec(memory_space=pltpu.VMEM), pl.BlockSpec(memory_space=pl.ANY)
    dma = pltpu.SemaphoreType.DMA
    hot_out, cold_out, cold_accum_out = pl.pallas_call(
        functools.partial(kernel, reps, shards),
        out_shape=(
            jax.ShapeDtypeStruct((2 * total, half_rows + PAD, LANES), f32),
            jax.ShapeDtypeStruct((cold_count, LANES), f32),
            jax.ShapeDtypeStruct((cold_count // LANES, 1, LANES), f32),
        ),
        in_specs=[vmem, vmem, anywhere, vmem, vmem, vmem, anywhere, vmem],
        out_specs=(vmem, vmem, vmem),
        scratch_shapes=[
            pltpu.VMEM((2, 2, reps, 1, half), i32),
            pltpu.VMEM((2, 2, reps, half, LANES), bf16),
            pltpu.VMEM((depth, own_rows, LANES), f32),
            pltpu.VMEM((max(depth - 1, 1), own_rows, LANES), f32),
            pltpu.VMEM((2, half_rows, LANES), f32),
            pltpu.VMEM((cold_count, LANES), f32),
            pltpu.VMEM((total, 1, LANES), i32),
            pltpu.VMEM((total, capacity, LANES), bf16),
            dma((4 * reps,)), dma((4 * reps,)), dma((4 * reps,)), dma((4 * reps,)),
            dma((depth,)), dma((depth,)), dma((depth,)), dma((depth,)),
            dma((2 * depth * reps,)), dma((2 * depth * reps,)),
            dma((1,)), dma((1,)), dma((2,)), dma((2,)), dma((4,)),
        ],
        compiler_params=pltpu.CompilerParams(collective_id=0, has_side_effects=True),
    )(
        hot_ids.reshape(2, 1, half),
        hot_grads.reshape(2, half, LANES),
        hot_rows.reshape(2 * total, half_rows, LANES),
        accum_blocks,
        cold_ids,
        cold_grads.reshape(total, capacity, LANES),
        cold_rows,
        cold_accum.reshape(cold_count // LANES, 1, LANES),
    )
    return (
        hot_out[:, :half_rows].reshape(hot_count, LANES),
        hot_out[:, half_rows, :half_rows].reshape(hot_count),
        cold_out,
        cold_accum_out.reshape(cold_count),
    )


def solution(mesh):
    placed = (
        P(BOTH), P(BOTH, None), P(), P(), P(BOTH, None), P(BOTH, None, None),
        P(BOTH, None, None, None), P(BOTH, None), P(BOTH),
    )
    return jax.shard_map(
        local,
        mesh=mesh,
        in_specs=placed,
        out_specs=(P(), P(), P(BOTH, None), P(BOTH)),
        check_vma=False,
    )
```

time: 200 us -> 90.6 us (0.45)
  waiting for transfers between devices: 116 us -> 0 us
  Pallas kernels: 0 us -> 77.6 us
  other arithmetic: 32.6 us -> 2.1 us
  blocking collectives: 23.2 us -> 0 us
  between operations: 13.8 us -> 0.68 us
  starting transfers between devices: 7.29 us -> 0 us
  local copies, waits for them, and re-layouts: 6.56 us -> 9.14 us
    pallas_call x0 -> x1, Pallas kernels: none -> 77.6 us  [local(): pl.pallas_call(functools.partial(kernel, reps, shards), out_shape=(jax.Sh...]
    reduce_scatter x1 -> x0, waiting for transfers between devices: 52.8 us -> none  [local(): part_sum = lax.psum_scatter(dense, 'shard', scatter_dimension=0, tiled=True)]
    psum x1 -> x0, waiting for transfers between devices: 46.8 us -> none  [local(): part_sum = lax.psum(part_sum, 'rep')]
    scatter-add x2 -> x0, other arithmetic: 18.7 us -> none  [the longest x1 14.1 us: local(): jax.ops.segment_sum(hot_grads.astype(jnp.float32), hot_ids, num_segments=...]
    all_to_all x2 -> x0, waiting for transfers between devices: 16.5 us -> none  [the longest x1 9.51 us: local(): lax.all_to_all(cold_grads, ('rep', 'shard'), split_axis=1, concat_axis=0,...]
    all_gather x1 -> x0, blocking collectives: 14.1 us -> none  [local(): lax.all_gather(accum_new, 'shard', axis=0, tiled=True)]
    all_to_all x1 -> x0, blocking collectives: 9.13 us -> none  [local(): lax.all_to_all(cold_slots, ('rep', 'shard'), split_axis=1, concat_axis=0,...]
    all_to_all x2 -> x0, starting transfers between devices: 7.18 us -> none  [the longest x1 4.6 us: local(): lax.all_to_all(cold_counts, ('rep', 'shard'), split_axis=1, concat_axis=0...]
  transfers between devices with their start and end apart: 5 -> 0, of which waited for: 4 -> 0; matrix products, arithmetic and copies ran while one was open for 8% -> 0% of each run, Pallas kernels for 0% -> 0%
where the time goes in v1:
time: 90.6 us; the launch traced here: 89.6 us
  Pallas kernels  77.6 us (86%)
  local copies, waits for them, and re-layouts  9.14 us (10%)
  other arithmetic  2.1 us (2%)
    pallas_call x1, Pallas kernels, local(): pl.pallas_call(functools.partial(kernel, reps, shards), out_shape=(jax.Sh...  77.6 us
    slice x1, local copies, waits for them, and re-layouts, local(): hot_out[:, :half_rows].reshape(hot_count, LANES)  4.86 us
    unnamed x6, local copies, waits for them, and re-layouts  2.64 us

profile of v1, /device:TPU:0, one launch (start us, length us, event | category | flops | bytes accessed | tf_op | source)
XLA Modules:
  0.0 89.6 jit_solution(13585538991837271714)
XLA Ops:
  0.7 0.7 add_bitcast_fusion
  1.4 0.1 copy.14
  1.4 1.4 %and_select_fusion.cold_ids = s32[32,1,128]{2,1,0:T(1,128)} fusion(s32[32,1,128]{2,1,0:T(1,128)S(1)} %copy.14, pred[128]{0:T(512)(128)(4,1)S(1)} %get-tuple-element.11, pred[128]{0:T(512)(128)(4,1)S(1)} %get-tuple-element.10, s32[32]{0:T(128)} %bitcast.23, s32[128]{0:T(128)S(1)} %get-tuple-element.13, s32[128]{0:T(128)S(1)} %get-tuple-element.14, ...), kind=kLoop, calls=%fused_computation | loop fusion | flops 24576 | bytes 35204 | tf_op jit(solution)/shard_map/jit(_where)/select_n | solution.py:307
  2.8 77.6 %shard_map.120 = (f32[64,136,128]{2,1,0:T(8,128)}, f32[8192,128]{1,0:T(8,128)}, f32[64,1,128]{2,1,0:T(1,128)}) custom-call(s32[2,1,1024]{2,1,0:T(1,128)} %bitcast.22, bf16[2,1024,128]{2,1,0:T(8,128)(2,1)} %bitcast.15, f32[64,128,128]{2,1,0:T(8,128)} %bitcast.14, f32[64,1,128]{2,1,0:T(1,128)} %bitcast.18, s32[32,1,128]{2,1,0:T(1,128)} %and_select_fusion.cold_ids, ...), custom_call_target="tpu_custom_call" | custom-call | tf_op jit(solution)/shard_map/pallas_call | solution.py:312
  80.5 1.6 %slice.7 = f32[64,1,128]{2,1,0:T(1,128)} slice(f32[64,136,128]{2,1,0:T(8,128)} %get-tuple-element.7), slice={[0:64], [128:129], [0:128]} | slice | bytes 65536 | tf_op jit(solution)/shard_map/slice | solution.py:348
  82.1 0.0 copy-start
  82.1 4.9 %slice.6 = f32[64,128,128]{2,1,0:T(8,128)} slice(f32[64,136,128]{2,1,0:T(8,128)} %get-tuple-element.7), slice={[0:64], [0:128], [0:128]} | slice | bytes 8388608 | tf_op jit(solution)/shard_map/slice | solution.py:347
  86.9 0.0 copy-done
  86.9 0.0 copy-start.1
  86.9 2.0 %copy.17 = f32[8192,128]{1,0:T(8,128)} copy(f32[8192,128]{1,0:T(8,128)S(1)} %copy-done) | data formatting | bytes 8388608
  88.9 0.0 copy-done.1
  88.9 0.6 copy.18
  (4 shorter events, 0.0 us)
Async XLA Ops:
  82.1 4.9 %copy-start = (f32[8192,128]{1,0:T(8,128)S(1)}, f32[8192,128]{1,0:T(8,128)}, u32[]{:S(2)}) copy-start(f32[8192,128]{1,0:T(8,128)} %get-tuple-element.22) | copy-start | bytes 12582916
  86.9 2.0 %copy-start.1 = (f32[64,1,128]{2,1,0:T(1,128)S(1)}, f32[64,1,128]{2,1,0:T(1,128)}, u32[]{:S(2)}) copy-start(f32[64,1,128]{2,1,0:T(1,128)} %get-tuple-element.9) | copy-start | bytes 98308

commit v2 on v1

--- a/solution.py
+++ b/solution.py
@@ -36,11 +36,11 @@
 def kernel(
     reps, shards,
     ids, grads, hot_rows, hot_accum, cold_ids, cold_grads, cold_rows, cold_accum,
-    hot_out, cold_out, cold_accum_out,
-    ids_buf, grads_buf, acc, z_buf, rows_buf, cold_buf, cids_buf, cgrads_buf,
+    hot_out, hot_accum_out, cold_out, cold_accum_out,
+    hot_buf, ids_buf, grads_buf, acc, z_buf, rows_buf, cold_buf, cids_buf, cgrads_buf,
     raw_send, raw_recv, raw_core_send, raw_core_recv, z_send, z_recv,
     zg_send, zg_recv, rg_send, rg_recv, core_send, core_recv,
-    cold_send, cold_recv, local_sem,
+    cold_send, cold_recv, local_sem, out_sem,
 ):
     total = reps * shards
     depth = shards // 2
@@ -55,6 +55,12 @@
     def flip(r, bit):
         m = 1 << bit
         return r + m * (1 - 2 * ((r // m) % 2))
+
+    def across(d):
+        r = 0
+        for k in range(depth.bit_length() - 1):
+            r += (1 << k) * ((z // (1 << k) + d // (1 << k)) % 2)
+        return r
 
     orders = (tuple(range(bits)), tuple(reversed(range(bits))))
 
@@ -174,7 +180,7 @@
 
             @pl.loop(1, depth + 1)
             def _(d):
-                zc = (z + d) % depth
+                zc = across(d % depth)
                 value = block_sum(c, i, (share + zc) * own_rows)
                 if i == 0 and c == 0:
                     acc[zc] = value
@@ -183,7 +189,7 @@
                 if last:
                     @pl.when(d >= 2)
                     def _():
-                        z_copy(d - 1, (z + d - 1) % depth).start()
+                        z_copy(d - 1, across(d - 1)).start()
 
     for copy in loads:
         copy.wait()
@@ -207,12 +213,15 @@
             new_rows, new_accum = adagrad(
                 cold_buf[at], cold_accum[2 * b + s], grad[s * LANES:(s + 1) * LANES]
             )
-            cold_out[at] = new_rows
+            cold_buf[at] = new_rows
             cold_accum_out[2 * b + s] = new_accum
+
+    cold_copy = pltpu.make_async_copy(cold_buf, cold_out, out_sem.at[0])
+    cold_copy.start()
 
     @pl.loop(1, depth)
     def _(d):
-        z_copy(d, (z + d) % depth).wait_recv()
+        z_copy(d, across(d)).wait_recv()
 
     for h in range(2):
         at = pl.ds(h * half_rows, half_rows)
@@ -220,12 +229,12 @@
         for d in range(1, depth):
             grad += z_buf[d - 1, at]
         new_rows, new_accum = adagrad(rows_buf[h], hot_accum[2 * chunk + h], grad)
-        hot_out[2 * chunk + h, pl.ds(0, half_rows)] = new_rows
-        hot_out[2 * chunk + h, pl.ds(half_rows, PAD)] = jnp.broadcast_to(new_accum, (PAD, LANES))
+        hot_buf[2 * chunk + h, pl.ds(0, half_rows)] = new_rows
+        hot_buf[2 * chunk + h, pl.ds(half_rows, PAD)] = jnp.broadcast_to(new_accum, (PAD, LANES))
 
     def zg_copy(d):
-        target = {"rep": rep, "shard": ((z + d) % depth) * 2 + core}
-        part = hot_out.at[pl.ds(2 * chunk, 2)]
+        target = {"rep": rep, "shard": across(d) * 2 + core}
+        part = hot_buf.at[pl.ds(2 * chunk, 2)]
         return remote(part, part, zg_send.at[d - 1], zg_recv.at[d - 1], target)
 
     for d in range(1, depth):
@@ -233,12 +242,17 @@
 
     gathered = {}
 
-    def out_block(d, h, i):
-        zc = (z + depth - d) % depth
-        return hot_out.at[2 * ((core * reps + origin(h, i)) * depth + zc) + h]
+    def out_block(d, h, i, side_of=core):
+        zc = across(d)
+        return 2 * ((side_of * reps + origin(h, i)) * depth + zc) + h
+
+    def publish(block):
+        pltpu.make_async_copy(
+            hot_buf.at[block, pl.ds(0, half_rows)], hot_out.at[block], out_sem.at[1]
+        ).start()
 
     def spread(d, h, i):
-        part = out_block(d, h, i)
+        part = hot_buf.at[out_block(d, h, i)]
         for q in range(top(i) + 1, bits):
             j = i | (1 << q)
             slot = (d * 2 + h) * reps + j
@@ -247,15 +261,28 @@
             copy.start()
             sends.append(copy)
             gathered[d, h, j] = copy
-        remote(part, part, core_send.at[0], core_recv.at[0], partner).start()
+        slot = (d * 2 + h) * reps + i
+        copy = remote(part, part, core_send.at[slot], core_recv.at[slot], partner)
+        copy.start()
+        sends.append(copy)
+        publish(out_block(d, h, i))
 
     def finish(d):
         for i in range(1, reps):
             for h in range(2):
-                part = out_block(d, h, i)
+                part = hot_buf.at[out_block(d, h, i)]
                 slot = (d * 2 + h) * reps + i
                 remote(part, part, rg_send.at[slot], rg_recv.at[slot], partner).wait_recv()
                 spread(d, h, i)
+
+    def crossed(d):
+        for i in range(reps):
+            for h in range(2):
+                block = out_block(d, h, i, 1 - core)
+                part = hot_buf.at[block]
+                slot = (d * 2 + h) * reps + i
+                remote(part, part, core_send.at[slot], core_recv.at[slot], partner).wait_recv()
+                publish(block)
 
     for d in range(depth):
         if d > 0:
@@ -264,21 +291,26 @@
             spread(d, h, 0)
         if d > 0:
             finish(d - 1)
+        if d > 1:
+            crossed(d - 2)
     finish(depth - 1)
+    for d in range(max(depth - 2, 0), depth):
+        crossed(d)
+
+    @pl.loop(0, 2 * total)
+    def _(b):
+        hot_accum_out[b] = hot_buf[b, pl.ds(half_rows, 1)]
 
     for copy in sends:
         copy.wait_send()
     for d in range(1, depth):
-        z_copy(d, (z + d) % depth).wait_send()
+        z_copy(d, across(d)).wait_send()
         zg_copy(d).wait_send()
     for k, buf in enumerate((cold_ids, cold_grads)):
         part = buf.at[pl.ds(0, total - 1)]
         pltpu.make_async_copy(part, part, cold_send.at[k]).wait()
-    side = reps * depth * 2
-    mine = hot_out.at[pl.ds(core * side, side)]
-    other = hot_out.at[pl.ds((1 - core) * side, side)]
-    pltpu.make_async_copy(mine, mine, core_send.at[0]).wait()
-    pltpu.make_async_copy(other, other, core_recv.at[0]).wait()
+    cold_copy.wait()
+    pltpu.make_async_copy(hot_out, hot_out, out_sem.at[1]).wait()
 
 
 def local(
@@ -286,7 +318,7 @@
 ):
     reps, shards = lax.axis_size("rep"), lax.axis_size("shard")
     total, depth = reps * shards, shards // 2
-    assert reps & (reps - 1) == 0 and shards % 2 == 0
+    assert reps & (reps - 1) == 0 and shards & (shards - 1) == 0
     hot_count, width = hot_rows.shape
     lookups = hot_ids.shape[0]
     own_rows = hot_count // total
@@ -309,16 +341,18 @@
     f32, i32, bf16 = jnp.float32, jnp.int32, jnp.bfloat16
     vmem, anywhere = pl.BlockSpec(memory_space=pltpu.VMEM), pl.BlockSpec(memory_space=pl.ANY)
     dma = pltpu.SemaphoreType.DMA
-    hot_out, cold_out, cold_accum_out = pl.pallas_call(
+    hot_out, hot_accum_out, cold_out, cold_accum_out = pl.pallas_call(
         functools.partial(kernel, reps, shards),
         out_shape=(
-            jax.ShapeDtypeStruct((2 * total, half_rows + PAD, LANES), f32),
+            jax.ShapeDtypeStruct((2 * total, half_rows, LANES), f32),
+            jax.ShapeDtypeStruct((2 * total, 1, LANES), f32),
             jax.ShapeDtypeStruct((cold_count, LANES), f32),
             jax.ShapeDtypeStruct((cold_count // LANES, 1, LANES), f32),
         ),
         in_specs=[vmem, vmem, anywhere, vmem, vmem, vmem, anywhere, vmem],
-        out_specs=(vmem, vmem, vmem),
+        out_specs=(anywhere, vmem, anywhere, vmem),
         scratch_shapes=[
+            pltpu.VMEM((2 * total, half_rows + PAD, LANES), f32),
             pltpu.VMEM((2, 2, reps, 1, half), i32),
             pltpu.VMEM((2, 2, reps, half, LANES), bf16),
             pltpu.VMEM((depth, own_rows, LANES), f32),
@@ -330,7 +364,8 @@
             dma((4 * reps,)), dma((4 * reps,)), dma((4 * reps,)), dma((4 * reps,)),
             dma((depth,)), dma((depth,)), dma((depth,)), dma((depth,)),
             dma((2 * depth * reps,)), dma((2 * depth * reps,)),
-            dma((1,)), dma((1,)), dma((2,)), dma((2,)), dma((4,)),
+            dma((2 * depth * reps,)), dma((2 * depth * reps,)),
+            dma((2,)), dma((2,)), dma((4,)), dma((2,)),
         ],
         compiler_params=pltpu.CompilerParams(collective_id=0, has_side_effects=True),
     )(
@@ -344,8 +379,8 @@
         cold_accum.reshape(cold_count // LANES, 1, LANES),
     )
     return (
-        hot_out[:, :half_rows].reshape(hot_count, LANES),
-        hot_out[:, half_rows, :half_rows].reshape(hot_count),
+        hot_out.reshape(hot_count, LANES),
+        hot_accum_out[:, 0, :half_rows].reshape(hot_count),
         cold_out,
         cold_accum_out.reshape(cold_count),
     )

time: 90.6 us -> 85.4 us (0.943)
  Pallas kernels: 77.6 us -> 74 us
  local copies, waits for them, and re-layouts: 9.14 us -> 7.94 us
    slice x2 -> x0, local copies, waits for them, and re-layouts: 6.44 us -> none  [the longest x1 4.86 us: local(): hot_out[:, :half_rows].reshape(hot_count, LANES)]
    unnamed x6 -> x10, local copies, waits for them, and re-layouts: 2.64 us -> 7.88 us
    pallas_call x1, Pallas kernels: 77.6 us -> 74 us  [local(): pl.pallas_call(functools.partial(kernel, reps, shards), out_shape=(jax.Sh...]
where the time goes in v2:
time: 85.4 us; the launch traced here: 84.7 us
  Pallas kernels  74 us (87%)
  local copies, waits for them, and re-layouts  7.94 us (9%)
  other arithmetic  2.1 us (2%)
    pallas_call x1, Pallas kernels, local(): pl.pallas_call(functools.partial(kernel, reps, shards), out_shape=(jax.Sh...  74 us
    unnamed x10, local copies, waits for them, and re-layouts  7.88 us

profile of v2, /device:TPU:0, one launch (start us, length us, event | category | flops | bytes accessed | tf_op | source)
XLA Modules:
  0.0 84.7 jit_solution(3037954233985548075)
XLA Ops:
  0.7 0.7 add_bitcast_fusion
  1.4 0.1 copy.14
  1.4 1.4 %and_select_fusion.cold_ids = s32[32,1,128]{2,1,0:T(1,128)} fusion(s32[32,1,128]{2,1,0:T(1,128)S(1)} %copy.14, pred[128]{0:T(512)(128)(4,1)S(1)} %get-tuple-element.13, pred[128]{0:T(512)(128)(4,1)S(1)} %get-tuple-element.12, s32[32]{0:T(128)} %bitcast.23, s32[128]{0:T(128)S(1)} %get-tuple-element.15, s32[128]{0:T(128)S(1)} %get-tuple-element.16, ...), kind=kLoop, calls=%fused_computation | loop fusion | flops 24576 | bytes 35204 | tf_op jit(solution)/shard_map/jit(_where)/select_n | solution.py:339
  2.8 74.0 %shard_map.120 = (f32[64,128,128]{2,1,0:T(8,128)}, f32[64,1,128]{2,1,0:T(1,128)}, f32[8192,128]{1,0:T(8,128)}, f32[64,1,128]{2,1,0:T(1,128)}) custom-call(s32[2,1,1024]{2,1,0:T(1,128)} %bitcast.22, bf16[2,1024,128]{2,1,0:T(8,128)(2,1)} %bitcast.15, f32[64,128,128]{2,1,0:T(8,128)} %bitcast.14, f32[64,1,128]{2,1,0:T(1,128)} %bitcast.18, ...), custom_call_target="tpu_custom_call" | custom-call | tf_op jit(solution)/shard_map/pallas_call | solution.py:344
  76.8 0.0 copy-start.2
  76.8 0.0 copy-start
  76.9 4.6 %copy.19 = f32[8192,128]{1,0:T(8,128)} copy(f32[8192,128]{1,0:T(8,128)} %bitcast.13) | data formatting | bytes 8388608
  81.5 0.0 copy-done.2
  81.5 0.6 copy.20
  82.1 0.0 copy-done
  82.1 0.0 copy-start.1
  82.1 2.0 %copy.21 = f32[8192,128]{1,0:T(8,128)} copy(f32[8192,128]{1,0:T(8,128)S(1)} %copy-done) | data formatting | bytes 8388608
  84.1 0.0 copy-done.1
  84.1 0.6 copy.22
  (4 shorter events, 0.0 us)
Async XLA Ops:
  76.8 4.6 %copy-start.2 = (f32[64,1,128]{2,1,0:T(1,128)S(1)}, f32[64,1,128]{2,1,0:T(1,128)}, u32[]{:S(2)}) copy-start(f32[64,1,128]{2,1,0:T(1,128)} %get-tuple-element.9) | copy-start | bytes 98308
  76.8 5.3 %copy-start = (f32[8192,128]{1,0:T(8,128)S(1)}, f32[8192,128]{1,0:T(8,128)}, u32[]{:S(2)}) copy-start(f32[8192,128]{1,0:T(8,128)} %get-tuple-element.24) | copy-start | bytes 12582916
  82.1 2.0 %copy-start.1 = (f32[64,1,128]{2,1,0:T(1,128)S(1)}, f32[64,1,128]{2,1,0:T(1,128)}, u32[]{:S(2)}) copy-start(f32[64,1,128]{2,1,0:T(1,128)} %get-tuple-element.11) | copy-start | bytes 98308
